TPU v7x, 32 devices: a whole 2x2x4 slice. The times are simulated.
32 devices in a mesh: dp: 4 (over x, core), fsdp: 4 (over z), mp: 2 (over y).
Axes of the slice: x: 2, y: 2, z: 4, core: 2. Of those that a mesh axis runs over, the one named last changes fastest.
Arguments:
- tokens_in: bfloat16 [4096, 3072], P(('dp', 'fsdp', 'mp')), may hold values from -40 to 40
- segment_ids: int32 [4096], P(('dp', 'fsdp', 'mp')), may hold values from 0 to 31, never falling along the last dimension, each value on 1 to 512 neighbouring positions
- target_ids: int32 [4096], P(('dp', 'fsdp', 'mp')), may hold values from 0 to 8191
- old_weights: bfloat16 [4, 3072, 2048], P(None, ('dp', 'fsdp', 'mp'))
- old_first: float32 [4, 3072, 2048], P(None, ('dp', 'fsdp', 'mp')), may hold values from -6 to 6
- old_second: float32 [4, 3072, 2048], P(None, ('dp', 'fsdp', 'mp')), may hold values from 0.01 to 4
- old_block: int32 [32], P(('dp', 'fsdp', 'mp')), may hold values from 0 to 31, each once
- new_residue: int32 [4], P('dp'), may hold values from 0 to 3, each once
- norm_gain: float32 [3072], replicated, may hold values from 0.5 to 1.5
- head_weight: bfloat16 [3072, 8192], P(None, ('fsdp', 'mp'))
Outputs:
- new_weights: bfloat16 [4, 3072, 2048], P(None, 'dp', ('fsdp', 'mp'))
- new_first: float32 [4, 3072, 2048], P(None, 'dp', ('fsdp', 'mp'))
- new_second: float32 [4, 3072, 2048], P(None, 'dp', ('fsdp', 'mp'))
- loss: float32 [4096], P(('dp', 'fsdp', 'mp'))
Inputs may be any that keep to these rules, and one draw needn't show every extreme that they name: `old_block`: a permutation of the old layout's row blocks. `new_residue`: a permutation; index i of dp holds the rows whose number modulo 4 is new_residue[i], in rising order. `segment_ids`: never falling along the tokens.
All inputs are finite; a program needn't handle non-finite values.
Results may differ from a plain program's by a relative error of at most 0.0075.
Values may be sent and summed in bfloat16 or wider, within the bound.
A program may use at most 192 MiB of HBM per device.

v0:
```python
import math
import jax
import jax.numpy as jnp
from jax import lax
from jax.sharding import PartitionSpec as P

HD = 128


def inverse_of(table):
    total_count = table.shape[0]
    places = jnp.arange(total_count, dtype=jnp.int32)
    return jnp.sum(jnp.where(table[None, :] == places[:, None], places[None, :], 0), axis=1)


def pack_rows(stored, residues, fm_count):
    matrices, row_count, columns = stored.shape
    dp_count = residues.shape[0]
    split_rows = stored.reshape(
        matrices, row_count // dp_count, dp_count, fm_count, columns // fm_count
    )
    chosen = jnp.take(split_rows, residues, axis=2, mode="clip")
    return chosen.transpose(2, 3, 0, 1, 4).reshape(
        dp_count * fm_count, matrices, row_count // dp_count, columns // fm_count
    )


def unpack_rows(received, holder):
    ordered = jnp.take(received, holder, axis=0, mode="clip")
    devices, matrices, pair_rows, group_cols = ordered.shape
    return ordered.transpose(1, 0, 2, 3).reshape(matrices, devices * pair_rows, group_cols)


def norm_rows(hidden, norm_gain):
    scale = lax.rsqrt(jnp.mean(hidden * hidden, axis=1, keepdims=True) + 1e-05)
    return (hidden * scale * norm_gain).astype(jnp.bfloat16)


FLAGS = dict(tail="a2a", first="before_rs", second="free", tokens="first")


def share_tables(segment_ids, target_ids, old_block, new_residue):
    axes = ("dp", "fsdp", "mp")
    own = jnp.concatenate([segment_ids, target_ids, old_block, new_residue])
    rows = jnp.broadcast_to(own[None, None], (lax.axis_size(axes), 1, own.shape[0]))
    rows = lax.all_to_all(rows, axes, split_axis=0, concat_axis=0, tiled=True)[:, 0]
    count = segment_ids.shape[0]
    fm_count = lax.axis_size(("fsdp", "mp"))
    here = lax.dynamic_slice_in_dim(rows, lax.axis_index("dp") * fm_count, fm_count)
    segments = here[:, :count].reshape(-1)
    targets = here[:, count : 2 * count].reshape(-1)
    return (segments, targets, rows[:, 2 * count], rows[::fm_count, 2 * count + 1])


def joint_loss(row_top, row_total, picked):
    axes = ("fsdp", "mp")
    fm_count = lax.axis_size(axes)
    parts = jnp.stack([row_top, row_total, picked])
    own_count = parts.shape[1] // fm_count
    if FLAGS["tail"] == "a2a":
        parts = parts.reshape(3, fm_count, own_count).transpose(1, 0, 2)
        parts = lax.all_to_all(parts, axes, split_axis=0, concat_axis=0, tiled=True)
    else:
        place = lax.axis_index(axes)
        rows = jnp.zeros((fm_count,) + parts.shape, jnp.float32)
        rows = lax.psum(lax.dynamic_update_slice(rows, parts[None], (place, 0, 0)), axes)
        parts = lax.dynamic_slice_in_dim(rows, place * own_count, own_count, axis=2)
    tops, totals, targets = (parts[:, 0], parts[:, 1], parts[:, 2])
    joint_max = jnp.max(tops, axis=0)
    joint_total = jnp.sum(totals * jnp.exp(tops - joint_max[None]), axis=0)
    return joint_max + jnp.log(joint_total) - jnp.sum(targets, axis=0)


def body(
    tokens_in,
    segment_ids,
    target_ids,
    old_weights,
    old_first,
    old_second,
    old_block,
    new_residue,
    norm_gain,
    head_weight,
):
    dp_count = lax.axis_size("dp")
    fm_count = lax.axis_size(("fsdp", "mp"))
    everyone = ("dp", "fsdp", "mp")
    columns = old_weights.shape[2]
    group_cols = columns // fm_count
    model_width = tokens_in.shape[1]
    new_rows = model_width // dp_count
    segments, targets, table_all, residues = share_tables(
        segment_ids, target_ids, old_block, new_residue
    )
    holder = inverse_of(table_all)
    inverse_res = inverse_of(residues)
    feature_ids = (
        residues[:, None] + dp_count * jnp.arange(new_rows, dtype=jnp.int32)[None]
    ).reshape(-1)
    logical_ids = (
        jnp.arange(new_rows, dtype=jnp.int32)[:, None] + new_rows * inverse_res[None]
    ).reshape(-1)
    own_picked = jnp.take(tokens_in, feature_ids, axis=1, mode="clip")
    picked_cols = lax.all_gather(own_picked, ("fsdp", "mp"), axis=0, tiled=True)
    seq_len = picked_cols.shape[0]
    weights_sent = pack_rows(old_weights, residues, fm_count)
    weights_got = lax.all_to_all(weights_sent, everyone, split_axis=0, concat_axis=0, tiled=True)
    first_sent = pack_rows(old_first, residues, fm_count)
    second_sent = pack_rows(old_second, residues, fm_count)
    if FLAGS["first"] != "free":
        weights_got, first_sent, second_sent = lax.optimization_barrier(
            (weights_got, first_sent, second_sent)
        )
    new_weights = unpack_rows(weights_got, holder)
    projections = new_weights[:3]
    if FLAGS.get("tokens") == "first":
        picked_cols, projections, first_sent = lax.optimization_barrier(
            (picked_cols, projections, first_sent)
        )
    first_got = lax.all_to_all(first_sent, everyone, split_axis=0, concat_axis=0, tiled=True)
    piece = lax.all_gather(projections, "dp", axis=1, tiled=True)
    projected = jnp.einsum("sr,mrc->msc", picked_cols, piece, preferred_element_type=jnp.float32)
    heads = group_cols // HD
    queries = projected[0].astype(jnp.bfloat16).reshape(seq_len, heads, HD)
    keys_all = projected[1].astype(jnp.bfloat16).reshape(seq_len, heads, HD)
    values_all = projected[2].astype(jnp.bfloat16).reshape(seq_len, heads, HD)
    positions_all = jnp.arange(seq_len, dtype=jnp.int32)
    allowed = (positions_all[:, None] >= positions_all[None, :]) & (
        segments[:, None] == segments[None, :]
    )
    scores = jnp.einsum("shd,thd->hst", queries, keys_all, preferred_element_type=jnp.float32) * (
        1.0 / math.sqrt(HD)
    )
    scores = jnp.where(allowed[None], scores, -1e30)
    row_max = jnp.max(scores, axis=2, keepdims=True)
    expo = jnp.where(allowed[None], jnp.exp(scores - row_max), 0.0)
    soft = (expo / jnp.sum(expo, axis=2, keepdims=True)).astype(jnp.bfloat16)
    attended = jnp.einsum("hst,thd->shd", soft, values_all, preferred_element_type=jnp.float32)
    attended = attended.astype(jnp.bfloat16).reshape(seq_len, group_cols)
    shuffled = jnp.einsum(
        "sc,rc->sr",
        attended,
        lax.all_gather(new_weights[3], "dp", axis=0, tiled=True),
        preferred_element_type=jnp.float32,
    )
    partial_value = shuffled.astype(jnp.bfloat16)
    if FLAGS["first"] == "rs_first":
        partial_value, second_sent = lax.optimization_barrier((partial_value, second_sent))
    if FLAGS["first"] == "before_rs":
        partial_value, first_got, second_sent = lax.optimization_barrier(
            (partial_value, first_got, second_sent)
        )
    second_got = lax.all_to_all(second_sent, everyone, split_axis=0, concat_axis=0, tiled=True)
    own_sum = lax.psum_scatter(partial_value, ("fsdp", "mp"), scatter_dimension=0, tiled=True)
    own_sum = jnp.take(own_sum, logical_ids, axis=1, mode="clip").astype(jnp.float32)
    own_normed = norm_rows(tokens_in.astype(jnp.float32) + own_sum, norm_gain)
    if FLAGS["second"] == "before_ag":
        own_normed, second_got = lax.optimization_barrier((own_normed, second_got))
    new_first = unpack_rows(first_got, holder)
    new_second = unpack_rows(second_got, holder)
    normed = lax.all_gather(own_normed, ("fsdp", "mp"), axis=0, tiled=True)
    logits = jnp.dot(normed, head_weight, preferred_element_type=jnp.float32)
    vocab_dev = logits.shape[1]
    offset = lax.axis_index(("fsdp", "mp")) * vocab_dev
    row_top = jnp.max(logits, axis=1)
    row_total = jnp.sum(jnp.exp(logits - row_top[:, None]), axis=1)
    vocab_ids = jnp.arange(vocab_dev, dtype=jnp.int32) + offset
    picked = jnp.sum(jnp.where(vocab_ids[None, :] == targets[:, None], logits, 0.0), axis=1)
    loss = joint_loss(row_top, row_total, picked)
    return (new_weights, new_first, new_second, loss)


def solution(mesh):
    placed = (
        P(("dp", "fsdp", "mp"), None),
        P(("dp", "fsdp", "mp")),
        P(("dp", "fsdp", "mp")),
        P(None, ("dp", "fsdp", "mp"), None),
        P(None, ("dp", "fsdp", "mp"), None),
        P(None, ("dp", "fsdp", "mp"), None),
        P(("dp", "fsdp", "mp")),
        P("dp"),
        P(),
        P(None, ("fsdp", "mp")),
    )
    return jax.shard_map(
        body,
        mesh=mesh,
        in_specs=placed,
        out_specs=(
            P(None, "dp", ("fsdp", "mp")),
            P(None, "dp", ("fsdp", "mp")),
            P(None, "dp", ("fsdp", "mp")),
            P(("dp", "fsdp", "mp")),
        ),
        check_vma=False,
    )
```

profile of v0, /device:TPU:0, one launch (start us, length us, event | category | flops | bytes accessed | tf_op | source)
XLA Modules:
  0.0 589.0 jit_solution(5896758327097351042)
XLA Ops:
  9.9 7.3 %all-to-all-start = ((s32[32,1,258]{2,1,0:T(1,128)}), s32[32,1,258]{2,1,0:T(1,128)S(1)}, u32[]{:S(2)}, u32[]{:S(2)}) async-start(s32[32,1,258]{2,1,0:T(1,128)} %broadcast_in_dim.85), calls=%async_computation | async-start | bytes 98304 | tf_op jit(solution)/shard_map/all_to_all | solution.py:46
  18.8 5.7 all-to-all-done
  24.7 11.4 %gather_fusion.4 = bf16[3072,128]{1,0:T(8,128)(2,1)} fusion(bf16[128,3072]{0,1:T(8,128)(2,1)S(1)} %copy.84, s32[3072]{0:T(1024)S(1)} %broadcast_clamp_fusion.1), kind=kCustom, calls=%fused_computation.4 | custom fusion | bytes 1585152 | tf_op jit(solution)/shard_map/jit(_take)/gather | solution.py:104
  45.9 5.1 copy.105
  54.2 4.3 gather_fusion.1
  58.5 4.5 copy.81
  63.0 4.4 gather_fusion.2
  67.4 4.6 copy.82
  72.2 34.0 %all-to-all-done.1 = bf16[32,4,24,256]{3,2,1,0:T(8,128)(2,1)S(1)} async-done(((bf16[32,4,24,256]{3,2,1,0:T(8,128)(2,1)}), bf16[32,4,24,256]{3,2,1,0:T(8,128)(2,1)S(1)}, u32[]{:S(2)}, u32[]{:S(2)}) %all-to-all-start.1) | async-done | bytes 1572896 | tf_op jit(solution)/shard_map/all_to_all | solution.py:108
  109.7 50.7 %all-gather.12.cloned.1.call-done = bf16[1024,3072]{0,1:T(8,128)(2,1)} async-done(((bf16[128,3072]{0,1:T(8,128)(2,1)}), bf16[1024,3072]{0,1:T(8,128)(2,1)}) %all-gather.12.cloned.1.call-update) | async-done | bytes 6291472 | tf_op jit(solution)/shard_map/all_gather | solution.py:105
  167.9 56.2 %all-gather.6.cloned.1.call-done = bf16[3,3072,256]{1,2,0:T(8,128)(2,1)} async-done(((bf16[3,768,256]{1,2,0:T(8,128)(2,1)}), bf16[3,3072,256]{1,2,0:T(8,128)(2,1)}) %all-gather.6.cloned.1.call-update) | async-done | bytes 4718608 | tf_op jit(solution)/shard_map/all_gather | solution.py:122
  224.1 8.5 %fusion.12 = bf16[3,1024,256]{1,2,0:T(8,128)(2,1)S(1)} fusion(bf16[3,3072,256]{1,2,0:T(8,128)(2,1)} %all-gather.6.cloned.1.call-done, bf16[1024,3072]{0,1:T(8,128)(2,1)} %all-gather.12.cloned.1.call-done), kind=kOutput, calls=%fused_computation.28 | convolution fusion | flops 4832624640 | bytes 12582912 | tf_op jit(solution)/shard_map/sr,mrc->msc/dot_general | solution.py:123
  233.9 8.7 %fusion.22 = (f32[2,1024]{1,0:T(2,128)S(1)}, f32[2,1024,1024]{1,2,0:T(8,128)}) fusion(pred[1024,1024]{0,1:T(8,128)(4,1)S(1)} %fusion.6, bf16[1024,2,128]{0,2,1:T(8,128)(2,1)} %bitcast.102, bf16[1024,2,128]{0,2,1:T(8,128)(2,1)} %bitcast.101), kind=kOutput, calls=%fused_computation.60 | convolution fusion | flops 547357696 | bytes 10493952 | tf_op jit(solution)/shard_map/sub | solution.py:137
  242.5 4.3 fusion.15
  250.7 5.9 %convolution_convert_fusion = bf16[1024,3072]{1,0:T(8,128)(2,1)} fusion(bf16[1024,256]{0,1:T(8,128)(2,1)S(1)} %bitcast.99, bf16[3072,256]{1,0:T(8,128)(2,1)} %all-gather.8.cloned.1.call-done), kind=kOutput, calls=%fused_computation.15 | convolution fusion | flops 1613758464 | bytes 8388608 | tf_op jit(solution)/shard_map/sc,rc->sr/dot_general | solution.py:141
  257.1 119.5 %reduce-scatter.2.cloned.1.call-done = bf16[128,3072]{1,0:T(8,128)(2,1)} async-done(((bf16[1024,3072]{1,0:T(8,128)(2,1)}), bf16[128,3072]{1,0:T(8,128)(2,1)}) %reduce-scatter.2.cloned.1.call-update) | async-done | bytes 786448 | tf_op jit(solution)/shard_map/reduce_scatter | solution.py:155
  378.0 11.5 %gather_fusion.7 = bf16[3072,128]{1,0:T(8,128)(2,1)} fusion(bf16[128,3072]{0,1:T(8,128)(2,1)S(1)} %copy.94, s32[3072]{0:T(1024)S(1)} %broadcast_clamp_fusion), kind=kCustom, calls=%fused_computation.7 | custom fusion | bytes 1585152 | tf_op jit(solution)/shard_map/jit(_take)/gather | solution.py:156
  393.7 4.2 all-to-all-start.3
  397.9 149.0 %all-gather.10.cloned.1.call-done = bf16[1024,3072]{0,1:T(8,128)(2,1)} async-done(((bf16[128,3072]{0,1:T(8,128)(2,1)}), bf16[1024,3072]{0,1:T(8,128)(2,1)}) %all-gather.10.cloned.1.call-update) | async-done | bytes 6291472 | tf_op jit(solution)/shard_map/all_gather | solution.py:162
  546.9 10.7 %fusion.23 = (f32[1024]{0:T(1024)S(1)}, f32[1024,1024]{0,1:T(8,128)S(1)}) fusion(bf16[1024,3072]{0,1:T(8,128)(2,1)} %all-gather.10.cloned.1.call-done, bf16[3072,1024]{1,0:T(8,128)(2,1)} %param.19), kind=kOutput, calls=%fused_computation.61 | convolution fusion | flops 6443498496 | bytes 16781312 | tf_op jit(solution)/shard_map/dot_general | solution.py:163
  559.7 4.7 all-to-all-start.4
  565.6 4.3 gather_fusion.5
  569.9 3.9 copy.91
  573.8 4.3 gather_fusion.6
  (70 shorter events, 45.9 us)
Async XLA Ops:
  9.9 14.6 %all-to-all-start = ((s32[32,1,258]{2,1,0:T(1,128)}), s32[32,1,258]{2,1,0:T(1,128)S(1)}, u32[]{:S(2)}, u32[]{:S(2)}) async-start(s32[32,1,258]{2,1,0:T(1,128)} %broadcast_in_dim.85), calls=%async_computation | async-start | bytes 98304 | tf_op jit(solution)/shard_map/all_to_all | solution.py:46
  17.2 143.2 %all-gather.12.cloned.1.call-start = ((), (), s32[]{:S(2)}) async-start(), calls=%async_computation.10 | async-start | bytes 7077888 | tf_op jit(solution)/shard_map/all_gather | solution.py:105
  24.4 11.8 %copy-start.2 = (s32[32,1,258]{2,1,0:T(1,128)}, s32[32,1,258]{2,1,0:T(1,128)S(1)}, u32[]{:S(2)}) copy-start(s32[32,1,258]{2,1,0:T(1,128)S(1)} %all-to-all-done) | copy-start | bytes 99076
  43.2 63.1 %all-to-all-start.1 = ((bf16[32,4,24,256]{3,2,1,0:T(8,128)(2,1)}), bf16[32,4,24,256]{3,2,1,0:T(8,128)(2,1)S(1)}, u32[]{:S(2)}, u32[]{:S(2)}) async-start(bf16[32,4,24,256]{3,2,1,0:T(8,128)(2,1)} %bitcast.1), calls=%async_computation.1 | async-start | bytes 3145728 | tf_op jit(solution)/shard_map/all_to_all | solution.py:108
  45.9 178.3 %all-gather.6.cloned.1.call-start = ((), (), s32[]{:S(2)}) async-start(), calls=%async_computation.6 | async-start | bytes 5898240 | tf_op jit(solution)/shard_map/all_gather | solution.py:122
  45.9 5.1 copy-start.1
  106.3 1.1 copy-start
  161.9 94.7 %all-to-all-start.2 = ((f32[32,4,24,256]{3,2,1,0:T(8,128)}), f32[32,4,24,256]{3,2,1,0:T(8,128)}, u32[]{:S(2)}, u32[]{:S(2)}) async-start(f32[32,4,24,256]{3,2,1,0:T(8,128)} %bitcast.81), calls=%async_computation.2 | async-start | bytes 6291456 | tf_op jit(solution)/shard_map/all_to_all | solution.py:121
  165.5 85.2 %all-gather.8.cloned.1.call-start = ((), (), s32[]{:S(2)}) async-start(), calls=%async_computation.7 | async-start | bytes 1966080 | tf_op jit(solution)/shard_map/all_gather | solution.py:144
  167.7 208.8 %reduce-scatter.2.cloned.1.call-start = ((), (), s32[]{:S(2)}) async-start(), calls=%async_computation.8 | async-start | bytes 7077888 | tf_op jit(solution)/shard_map/reduce_scatter | solution.py:155
  256.6 290.3 %all-gather.10.cloned.1.call-start = ((), (), s32[]{:S(2)}) async-start(), calls=%async_computation.9 | async-start | bytes 7077888 | tf_op jit(solution)/shard_map/all_gather | solution.py:162
  378.0 13.1 %copy-start.3 = (f32[3072]{0:T(1024)S(1)}, f32[3072]{0:T(1024)}, u32[]{:S(2)}) copy-start(f32[3072]{0:T(1024)} %param.18) | copy-start | bytes 36868
  393.7 166.0 %all-to-all-start.3 = ((f32[32,4,24,256]{3,2,1,0:T(8,128)}), f32[32,4,24,256]{3,2,1,0:T(8,128)}, u32[]{:S(2)}, u32[]{:S(2)}) async-start(f32[32,4,24,256]{3,2,1,0:T(8,128)} %bitcast.80), calls=%async_computation.3 | async-start | bytes 6291456 | tf_op jit(solution)/shard_map/all_to_all | solution.py:154
  559.7 22.3 %all-to-all-start.4 = ((f32[8,3,128]{2,1,0:T(4,128)}), f32[8,3,128]{2,1,0:T(4,128)S(1)}, u32[]{:S(2)}, u32[]{:S(2)}) async-start(f32[8,3,128]{2,1,0:T(4,128)} %maximum_bitcast_fusion), calls=%async_computation.5 | async-start | bytes 32768 | tf_op jit(solution)/shard_map/all_to_all | solution.py:62
Sparse Core Ops, SparseCore 0:
  36.3 124.0 all-gather.11
  162.5 61.5 all-gather.5
  225.7 24.9 all-gather.7
  256.7 119.7 reduce-scatter.1
  393.8 153.0 all-gather.9
where the time goes:
time: 590 us; the launch traced here: 589 us
  waiting for transfers between devices  419 us (71%)
  local copies, waits for them, and re-layouts  85.3 us (14%)
  matrix products  38.1 us (6%)
  starting transfers between devices  22.9 us (4%)
  between operations  15.3 us (3%)
  other arithmetic  8.52 us (1%)
    all_gather x1, waiting for transfers between devices, body(): normed = lax.all_gather(own_normed, ('fsdp', 'mp'), axis=0, tiled=True)  149 us
    reduce_scatter x1, waiting for transfers between devices, body(): lax.psum_scatter(partial_value, ('fsdp', 'mp'), scatter_dimension=0, tile...  119 us
    all_gather x1, waiting for transfers between devices, body(): piece = lax.all_gather(projections, 'dp', axis=1, tiled=True)  56.2 us
    all_gather x1, waiting for transfers between devices, body(): picked_cols = lax.all_gather(own_picked, ('fsdp', 'mp'), axis=0, tiled=True)  50.7 us
    all_to_all x1, waiting for transfers between devices, body(): lax.all_to_all(weights_sent, everyone, split_axis=0, concat_axis=0, tiled...  34 us
    unnamed x14, local copies, waits for them, and re-layouts  12.8 us
    transpose x3, local copies, waits for them, and re-layouts, pack_rows(): chosen.transpose(2, 3, 0, 1, 4)  12.3 us
  transfers between devices with their start and end apart: 10, of which 7 were waited for; matrix products, arithmetic and copies ran while one was open for 17% of the time, Pallas kernels for 0%

commit v1 on v0

--- a/solution.py
+++ b/solution.py
@@ -119,7 +119,7 @@
             (picked_cols, projections, first_sent)
         )
     first_got = lax.all_to_all(first_sent, everyone, split_axis=0, concat_axis=0, tiled=True)
-    piece = lax.all_gather(projections, "dp", axis=1, tiled=True)
+    piece = jnp.concatenate(lax.all_gather(projections, "dp"), axis=1)
     projected = jnp.einsum("sr,mrc->msc", picked_cols, piece, preferred_element_type=jnp.float32)
     heads = group_cols // HD
     queries = projected[0].astype(jnp.bfloat16).reshape(seq_len, heads, HD)

time: 590 us -> 600 us (1.017)
  local copies, waits for them, and re-layouts: 85.3 us -> 94.7 us
    reshape x0 -> x2, local copies, waits for them, and re-layouts: none -> 17.8 us  [body(): piece = jnp.concatenate(lax.all_gather(projections, 'dp'), axis=1)]
    unnamed x14 -> x12, local copies, waits for them, and re-layouts: 12.8 us -> 12.8 us
  transfers between devices with their start and end apart: 10 -> 10, of which waited for: 7 -> 6; matrix products, arithmetic and copies ran while one was open for 17% -> 18% of each run, Pallas kernels for 0% -> 0%
where the time goes in v1:
time: 600 us; the launch traced here: 598 us
  waiting for transfers between devices  419 us (70%)
  local copies, waits for them, and re-layouts  94.7 us (16%)
  matrix products  38.1 us (6%)
  starting transfers between devices  22.8 us (4%)
  between operations  15.3 us (3%)
  other arithmetic  8.51 us (1%)
    all_gather x1, waiting for transfers between devices, body(): normed = lax.all_gather(own_normed, ('fsdp', 'mp'), axis=0, tiled=True)  149 us
    reduce_scatter x1, waiting for transfers between devices, body(): lax.psum_scatter(partial_value, ('fsdp', 'mp'), scatter_dimension=0, tile...  123 us
    all_gather x1, waiting for transfers between devices, body(): piece = jnp.concatenate(lax.all_gather(projections, 'dp'), axis=1)  56.9 us
    all_gather x1, waiting for transfers between devices, body(): picked_cols = lax.all_gather(own_picked, ('fsdp', 'mp'), axis=0, tiled=True)  49.7 us
    all_to_all x1, waiting for transfers between devices, body(): lax.all_to_all(weights_sent, everyone, split_axis=0, concat_axis=0, tiled...  34.1 us
    reshape x2, local copies, waits for them, and re-layouts, body(): piece = jnp.concatenate(lax.all_gather(projections, 'dp'), axis=1)  17.8 us
    unnamed x12, local copies, waits for them, and re-layouts  12.8 us
    transpose x3, local copies, waits for them, and re-layouts, pack_rows(): chosen.transpose(2, 3, 0, 1, 4)  12.2 us
  transfers between devices with their start and end apart: 10, of which 6 were waited for; matrix products, arithmetic and copies ran while one was open for 18% of the time, Pallas kernels for 0%

profile of v1, /device:TPU:0, one launch (start us, length us, event | category | flops | bytes accessed | tf_op | source)
XLA Modules:
  0.0 598.2 jit_solution(15395369048747787468)
XLA Ops:
  9.9 7.3 %all-to-all-start = ((s32[32,1,258]{2,1,0:T(1,128)}), s32[32,1,258]{2,1,0:T(1,128)S(1)}, u32[]{:S(2)}, u32[]{:S(2)}) async-start(s32[32,1,258]{2,1,0:T(1,128)} %broadcast_in_dim.85), calls=%async_computation | async-start | bytes 98304 | tf_op jit(solution)/shard_map/all_to_all | solution.py:46
  18.8 5.7 all-to-all-done
  24.7 11.4 %gather_fusion.4 = bf16[3072,128]{1,0:T(8,128)(2,1)} fusion(bf16[128,3072]{0,1:T(8,128)(2,1)S(1)} %copy.82, s32[3072]{0:T(1024)S(1)} %broadcast_clamp_fusion.1), kind=kCustom, calls=%fused_computation.4 | custom fusion | bytes 1585152 | tf_op jit(solution)/shard_map/jit(_take)/gather | solution.py:104
  45.9 5.1 copy.103
  54.1 4.3 gather_fusion.1
  58.5 4.5 copy.79
  63.0 4.4 gather_fusion.2
  67.4 4.5 copy.80
  72.1 34.1 %all-to-all-done.1 = bf16[32,4,24,256]{3,2,1,0:T(8,128)(2,1)S(1)} async-done(((bf16[32,4,24,256]{3,2,1,0:T(8,128)(2,1)}), bf16[32,4,24,256]{3,2,1,0:T(8,128)(2,1)S(1)}, u32[]{:S(2)}, u32[]{:S(2)}) %all-to-all-start.1) | async-done | bytes 1572896 | tf_op jit(solution)/shard_map/all_to_all | solution.py:108
  110.7 49.7 %all-gather.11.cloned.1.call-done = bf16[1024,3072]{0,1:T(8,128)(2,1)} async-done(((bf16[128,3072]{0,1:T(8,128)(2,1)}), bf16[1024,3072]{0,1:T(8,128)(2,1)}) %all-gather.11.cloned.1.call-update) | async-done | bytes 6291472 | tf_op jit(solution)/shard_map/all_gather | solution.py:105
  160.4 3.5 all-to-all-start.2
  165.7 56.9 %all-gather.13.cloned.1.call-done = bf16[12,768,256]{2,1,0:T(8,128)(2,1)} async-done(((bf16[3,768,256]{2,1,0:T(8,128)(2,1)}), bf16[12,768,256]{2,1,0:T(8,128)(2,1)}) %all-gather.13.cloned.1.call-update) | async-done | bytes 4718608 | tf_op jit(solution)/shard_map/all_gather | solution.py:122
  222.6 8.4 %copy.84 = bf16[3,4,768,256]{2,1,3,0:T(4,128)(2,1)} copy(bf16[3,4,768,256]{3,2,0,1:T(8,128)(2,1)} %bitcast.95) | data formatting | bytes 9437184 | tf_op jit(solution)/shard_map/reshape | solution.py:122
  231.0 9.4 %reshape.198 = bf16[3,3072,256]{1,2,0:T(8,128)(2,1)} reshape(bf16[3,4,768,256]{2,1,3,0:T(4,128)(2,1)} %copy.84) | data formatting | bytes 9437184 | tf_op jit(solution)/shard_map/reshape | solution.py:122
  240.4 8.6 %fusion.12 = bf16[3,1024,256]{1,2,0:T(8,128)(2,1)S(1)} fusion(bf16[3,3072,256]{1,2,0:T(8,128)(2,1)} %reshape.198, bf16[1024,3072]{0,1:T(8,128)(2,1)} %all-gather.11.cloned.1.call-done), kind=kOutput, calls=%fused_computation.28 | convolution fusion | flops 4832624640 | bytes 12582912 | tf_op jit(solution)/shard_map/sr,mrc->msc/dot_general | solution.py:123
  250.2 8.7 %fusion.22 = (f32[2,1024]{1,0:T(2,128)S(1)}, f32[2,1024,1024]{1,2,0:T(8,128)}) fusion(pred[1024,1024]{0,1:T(8,128)(4,1)S(1)} %fusion.6, bf16[1024,2,128]{0,2,1:T(8,128)(2,1)} %bitcast.108, bf16[1024,2,128]{0,2,1:T(8,128)(2,1)} %bitcast.107), kind=kOutput, calls=%fused_computation.60 | convolution fusion | flops 547357696 | bytes 10493952 | tf_op jit(solution)/shard_map/sub | solution.py:137
  258.8 4.3 fusion.15
  263.2 5.9 convolution_convert_fusion
  269.6 123.3 %reduce-scatter.2.cloned.1.call-done = bf16[128,3072]{1,0:T(8,128)(2,1)} async-done(((bf16[1024,3072]{1,0:T(8,128)(2,1)}), bf16[128,3072]{1,0:T(8,128)(2,1)}) %reduce-scatter.2.cloned.1.call-update) | async-done | bytes 786448 | tf_op jit(solution)/shard_map/reduce_scatter | solution.py:155
  394.4 11.5 %gather_fusion.7 = bf16[3072,128]{1,0:T(8,128)(2,1)} fusion(bf16[128,3072]{0,1:T(8,128)(2,1)S(1)} %copy.92, s32[3072]{0:T(1024)S(1)} %broadcast_clamp_fusion), kind=kCustom, calls=%fused_computation.7 | custom fusion | bytes 1585152 | tf_op jit(solution)/shard_map/jit(_take)/gather | solution.py:156
  410.0 4.2 all-to-all-start.3
  414.2 149.0 %all-gather.9.cloned.1.call-done = bf16[1024,3072]{0,1:T(8,128)(2,1)} async-done(((bf16[128,3072]{0,1:T(8,128)(2,1)}), bf16[1024,3072]{0,1:T(8,128)(2,1)}) %all-gather.9.cloned.1.call-update) | async-done | bytes 6291472 | tf_op jit(solution)/shard_map/all_gather | solution.py:162
  563.2 10.7 %fusion.23 = (f32[1024]{0:T(1024)S(1)}, f32[1024,1024]{0,1:T(8,128)S(1)}) fusion(bf16[1024,3072]{0,1:T(8,128)(2,1)} %all-gather.9.cloned.1.call-done, bf16[3072,1024]{1,0:T(8,128)(2,1)} %param.19), kind=kOutput, calls=%fused_computation.61 | convolution fusion | flops 6443498496 | bytes 16781312 | tf_op jit(solution)/shard_map/dot_general | solution.py:163
  575.9 4.7 all-to-all-start.4
  (69 shorter events, 42.7 us)
Async XLA Ops:
  9.9 14.6 %all-to-all-start = ((s32[32,1,258]{2,1,0:T(1,128)}), s32[32,1,258]{2,1,0:T(1,128)S(1)}, u32[]{:S(2)}, u32[]{:S(2)}) async-start(s32[32,1,258]{2,1,0:T(1,128)} %broadcast_in_dim.85), calls=%async_computation | async-start | bytes 98304 | tf_op jit(solution)/shard_map/all_to_all | solution.py:46
  17.2 143.2 %all-gather.11.cloned.1.call-start = ((), (), s32[]{:S(2)}) async-start(), calls=%async_computation.9 | async-start | bytes 7077888 | tf_op jit(solution)/shard_map/all_gather | solution.py:105
  43.1 63.1 %all-to-all-start.1 = ((bf16[32,4,24,256]{3,2,1,0:T(8,128)(2,1)}), bf16[32,4,24,256]{3,2,1,0:T(8,128)(2,1)S(1)}, u32[]{:S(2)}, u32[]{:S(2)}) async-start(bf16[32,4,24,256]{3,2,1,0:T(8,128)(2,1)} %bitcast.1), calls=%async_computation.1 | async-start | bytes 3145728 | tf_op jit(solution)/shard_map/all_to_all | solution.py:108
  45.8 176.7 %all-gather.13.cloned.1.call-start = ((), (), s32[]{:S(2)}) async-start(), calls=%async_computation.10 | async-start | bytes 5898240 | tf_op jit(solution)/shard_map/all_gather | solution.py:122
  45.9 5.1 copy-start.1
  106.2 1.1 copy-start
  160.4 108.7 %all-to-all-start.2 = ((f32[32,4,24,256]{3,2,1,0:T(8,128)}), f32[32,4,24,256]{3,2,1,0:T(8,128)}, u32[]{:S(2)}, u32[]{:S(2)}) async-start(f32[32,4,24,256]{3,2,1,0:T(8,128)} %bitcast.86), calls=%async_computation.2 | async-start | bytes 6291456 | tf_op jit(solution)/shard_map/all_to_all | solution.py:121
  163.9 99.2 %all-gather.7.cloned.1.call-start = ((), (), s32[]{:S(2)}) async-start(), calls=%async_computation.6 | async-start | bytes 1966080 | tf_op jit(solution)/shard_map/all_gather | solution.py:144
  165.5 227.4 %reduce-scatter.2.cloned.1.call-start = ((), (), s32[]{:S(2)}) async-start(), calls=%async_computation.7 | async-start | bytes 7077888 | tf_op jit(solution)/shard_map/reduce_scatter | solution.py:155
  269.1 294.1 %all-gather.9.cloned.1.call-start = ((), (), s32[]{:S(2)}) async-start(), calls=%async_computation.8 | async-start | bytes 7077888 | tf_op jit(solution)/shard_map/all_gather | solution.py:162
  394.3 13.1 %copy-start.2 = (f32[3072]{0:T(1024)S(1)}, f32[3072]{0:T(1024)}, u32[]{:S(2)}) copy-start(f32[3072]{0:T(1024)} %param.18) | copy-start | bytes 36868
  410.0 166.0 %all-to-all-start.3 = ((f32[32,4,24,256]{3,2,1,0:T(8,128)}), f32[32,4,24,256]{3,2,1,0:T(8,128)}, u32[]{:S(2)}, u32[]{:S(2)}) async-start(f32[32,4,24,256]{3,2,1,0:T(8,128)} %bitcast.85), calls=%async_computation.3 | async-start | bytes 6291456 | tf_op jit(solution)/shard_map/all_to_all | solution.py:154
  575.9 15.2 %all-to-all-start.4 = ((f32[8,3,128]{2,1,0:T(4,128)}), f32[8,3,128]{2,1,0:T(4,128)S(1)}, u32[]{:S(2)}, u32[]{:S(2)}) async-start(f32[8,3,128]{2,1,0:T(4,128)} %maximum_bitcast_fusion), calls=%async_computation.5 | async-start | bytes 32768 | tf_op jit(solution)/shard_map/all_to_all | solution.py:62
Sparse Core Ops, SparseCore 0:
  36.3 124.0 all-gather.10
  162.5 60.0 all-gather.12
  224.1 25.1 all-gather.6
  269.2 123.5 reduce-scatter.1
  410.1 153.0 all-gather.8
